TPU v7x, 256 devices: a 4x2x16 block of a 4x16x16 slice. The times are simulated.
256 devices in a mesh: grp: 2 (over y), slab: 32 (over z, core), ang: 4 (over x).
Axes of the slice: x: 4, y: 2, z: 16, core: 2. Of those that a mesh axis runs over, the one named last changes fastest.
The devices are a block of a 4x16x16 slice.
Arguments:
- volume: bfloat16 [128, 256, 1024], P(('grp', 'slab')), parts along dimension 0, may hold values from -6 to 6
- ray_weights: bfloat16 [8, 1024, 1024], P('ang'), may hold values from -0.0234375 to 0.0234375
- row_offsets: int32 [8, 64], P('ang'), may hold values from 0 to 8
- measured: float32 [16, 256, 1024], P(('grp', 'ang'), 'slab'), parts along dimension 0, may hold values from -6 to 6
- shifts: float32 [16], P(('grp', 'ang')), parts along dimension 0, may hold values from -4 to 4
Outputs:
- updated_volume: bfloat16 [128, 256, 1024], P(('grp', 'slab')), parts along dimension 0
- last_residual: float32 [16, 256, 1024], P(('grp', 'ang'), 'slab'), parts along dimension 0
- shift_slope: float32 [16], P(('grp', 'ang')), parts along dimension 0
There are 2 independent parts, one for each index of `grp`. A program takes and returns all parts, laid end to end along the dimension named above; an argument that names none is the same for every part. Nothing has to cross between parts.
All inputs are finite; a program needn't handle non-finite values.
Results may differ from a plain program's by a relative error of at most 0.006.
Values may be sent and summed in bfloat16 or wider, within the bound.
No kernel may reach another device: no remote copies, remote signals or barrier semaphores. Data moves between devices by JAX's collectives and lax.ppermute only.
A program may use at most 128 MiB of HBM per device.

v0:
```python
import math
import jax
import jax.numpy as jnp
from jax import lax
from jax.sharding import Mesh
from jax.sharding import PartitionSpec as P

Y = 256
X = 1024
U = 1024
OFF = 8
ROUNDS = 2
SLAB = ("slab_0", "slab_1")
GRP_SLAB = ("grp", "slab_0", "slab_1")
step_size = 0.5


def own_block(tiles, axes, order):
    lengths = [lax.axis_size(a) for a in axes]
    tiles = tiles.reshape(*lengths, *tiles.shape[1:])
    tiles = tiles.transpose(*order, *range(len(axes), tiles.ndim))
    tiles = tiles.reshape(-1, *tiles.shape[len(axes) :])
    for k in order:
        tiles = lax.psum_scatter(tiles, axes[k], scatter_dimension=0, tiled=True)
    return tiles[0]


def in_blocks(shard, dim, length):
    lengths = shard.shape
    tiles = shard.reshape(*lengths[:dim], length, lengths[dim] // length, *lengths[dim + 1 :])
    return jnp.moveaxis(tiles, dim, 0)


def summed_rows(shard, axes, order, dim):
    length = lax.axis_size(axes)
    return own_block(in_blocks(shard, dim, length), axes, order)


def in_order(tiles, dim):
    lengths = list(tiles.shape[1:])
    lengths[dim] *= tiles.shape[0]
    return jnp.moveaxis(tiles, 0, dim).reshape(lengths)


def stacked_from(shard, axes, order):
    tiles = shard
    for k in order:
        tiles = lax.all_gather(tiles, axes[k])
    done = order[::-1]
    back = [done.index(k) for k in range(len(axes))]
    tiles = tiles.transpose(*back, *range(len(axes), tiles.ndim))
    return tiles.reshape(-1, *shard.shape)


def gather_axes(shard, axes, order, dim):
    return in_order(stacked_from(shard, axes, order), dim)


def from_everyone(shard, axis):
    copies = jnp.broadcast_to(shard, (lax.axis_size(axis), *shard.shape))
    return lax.all_to_all(copies, axis, split_axis=0, concat_axis=0, tiled=True)


def over_copies(shard, axis):
    return from_everyone(shard, axis).sum(axis=0)


def move_down(products, tilt_table):
    base = jnp.zeros((products.shape[1] + OFF, U), jnp.float32)
    placed = jax.vmap(
        lambda block, shift_rows: lax.dynamic_update_slice(base, block, (shift_rows, jnp.int32(0)))
    )(products, tilt_table)
    return jnp.sum(placed, axis=0)


def backproject(extended, tilt_table, ray_weights, band_rows):
    slices_count = tilt_table.shape[1]
    running = jnp.zeros((slices_count * band_rows, X), jnp.float32)
    for angle_index in range(ray_weights.shape[0]):
        source = extended[angle_index]
        picked = jax.vmap(
            lambda shift_rows: lax.dynamic_slice(source, (shift_rows, jnp.int32(0)), (band_rows, U))
        )(tilt_table[angle_index])
        running = running + lax.dot_general(
            picked.reshape(slices_count * band_rows, U),
            ray_weights[angle_index],
            (((1,), (1,)), ((), ())),
            preferred_element_type=jnp.float32,
        )
    return running


def apply_update(current, running):
    partial_value = lax.optimization_barrier(running.reshape(current.shape).astype(jnp.bfloat16))
    partial_wide = partial_value.astype(jnp.float32)
    gradient = lax.psum(partial_wide, "ang")
    renewed = (current.astype(jnp.float32) - step_size * gradient).astype(jnp.bfloat16)
    return renewed


def per_device(volume, ray_weights, row_offsets, measured, shifts):
    angles_here = ray_weights.shape[0]
    band_rows = measured.shape[1]
    highest = lax.Precision.HIGHEST
    numbers = lax.iota(jnp.int32, U)
    turns = numbers[:, None] * numbers[None, :] % U
    radians = turns.astype(jnp.float32) * (2.0 * math.pi / U)
    cosine = jnp.cos(radians)
    sine = jnp.sin(radians)
    signed = jnp.where(numbers <= (U - 1) // 2, numbers, numbers - U)
    omega = signed.astype(jnp.float32) * (2.0 * math.pi / U)
    flat_rows = measured.reshape(angles_here * band_rows, U)
    real_part = jnp.dot(flat_rows, cosine, precision=highest).reshape(angles_here, band_rows, U)
    imag_part = -jnp.dot(flat_rows, sine, precision=highest).reshape(angles_here, band_rows, U)
    phase = omega[None, None, :] * shifts[:, None, None]
    turned_real = real_part * jnp.cos(phase) + imag_part * jnp.sin(phase)
    turned_imag = imag_part * jnp.cos(phase) - real_part * jnp.sin(phase)
    first_half = jnp.concatenate([turned_real, omega * turned_imag], axis=0).reshape(-1, U)
    second_half = jnp.concatenate([turned_imag, -omega * turned_real], axis=0).reshape(-1, U)
    inverse = (
        jnp.dot(first_half, cosine, precision=highest)
        - jnp.dot(second_half, sine, precision=highest)
    ) / U
    inverse = inverse.reshape(2, angles_here, band_rows, U)
    shifted = inverse[0]
    slope_field = inverse[1]
    projection = shifted
    residual = shifted
    current = volume
    slices_here = volume.shape[0]
    tilt_table = lax.dynamic_slice_in_dim(
        row_offsets, lax.axis_index(SLAB) * slices_here, slices_here, 1
    )
    for round_index in range(ROUNDS):
        flattened = current.reshape(slices_here * Y, X)
        partials = jnp.stack(
            [
                move_down(
                    jnp.dot(
                        flattened, ray_weights[angle_index], preferred_element_type=jnp.float32
                    ).reshape(slices_here, Y, U),
                    tilt_table[angle_index],
                )[:Y]
                for angle_index in range(angles_here)
            ]
        )
        projection = summed_rows(partials, SLAB, (1, 0), 1)
        residual = projection - shifted
        rounded = residual.astype(jnp.bfloat16)
        gathered = gather_axes(rounded, SLAB, (0, 1), 1)
        extended = jnp.concatenate(
            [gathered, jnp.zeros((angles_here, OFF, U), jnp.bfloat16)], axis=1
        )
        running = backproject(extended, tilt_table, ray_weights, Y)
        current = apply_update(current, running)
    local_dot = jnp.sum(projection * slope_field, axis=(1, 2))
    shift_slope = over_copies(local_dot, SLAB) / math.sqrt(Y * U)
    return (current, residual, shift_slope)


def solution(mesh):
    split = Mesh(
        mesh.devices.reshape(mesh.shape["grp"], 16, 2, mesh.shape["ang"]),
        ("grp", "slab_0", "slab_1", "ang"),
    )
    placed = (
        P(GRP_SLAB, None, None),
        P("ang", None, None),
        P("ang", None),
        P(("grp", "ang"), SLAB, None),
        P(("grp", "ang")),
    )
    return jax.shard_map(
        per_device,
        mesh=split,
        in_specs=placed,
        out_specs=(P(GRP_SLAB, None, None), P(("grp", "ang"), SLAB, None), P(("grp", "ang"))),
        check_vma=False,
    )
```

profile of v0, /device:TPU:34, one launch (start us, length us, event | category | flops | bytes accessed | tf_op | source)
XLA Modules:
  0.0 536.4 jit_solution(7147799609888639398)
XLA Ops:
  7.3 4.7 fusion.16
  15.2 18.0 %while.12 = (s32[]{:T(128)}, f32[2,264,1024]{2,1,0:T(8,128)S(1)}, s32[2,3]{1,0:T(2,128)S(1)}, f32[2,256,1024]{2,1,0:T(8,128)}, s32[]{:T(128)}, /*index=5*/s32[3]{0:T(128)S(1)}, s32[]{:T(128)}) while((s32[]{:T(128)}, f32[2,264,1024]{2,1,0:T(8,128)S(1)}, s32[2,3]{1,0:T(2,128)S(1)}, f32[2,256,1024]{2,1,0:T(8,128)}, s32[]{:T(128)}, ...), condition=%wide.while_cond.4, body=%wide.while_body.4.sunk | while | flops 262163 | bytes 5243051 | solution.py:71
  18.7 3.4 dynamic-slice_select_fusion.8
  27.7 3.4 dynamic-slice_select_fusion.8
  34.9 24.1 %while.13 = (s32[]{:T(128)}, f32[2,264,1024]{2,1,0:T(8,128)}, s32[2,3]{1,0:T(2,128)S(1)}, f32[2,256,1024]{2,1,0:T(8,128)}, s32[]{:T(128)}, /*index=5*/s32[3]{0:T(128)S(1)}, s32[]{:T(128)}) while((s32[]{:T(128)}, f32[2,264,1024]{2,1,0:T(8,128)}, s32[2,3]{1,0:T(2,128)S(1)}, f32[2,256,1024]{2,1,0:T(8,128)}, s32[]{:T(128)}, /*index=5*/s32[3]{0:T(128)S(1)}, ...), condition=%wide.while_cond.5, body=%wide.while_body.5.sunk | while | flops 262163 | bytes 5243051 | solution.py:71
  38.3 3.6 dynamic-slice_select_fusion.9
  41.9 5.1 dynamic-update-slice.33
  50.3 3.6 dynamic-slice_select_fusion.9
  53.9 5.1 dynamic-update-slice.33
  63.3 32.5 %reduce-scatter.5.cloned.1.call-done = f32[16,2,8,1024]{3,2,1,0:T(8,128)} async-done(((f32[32,2,8,1024]{3,2,1,0:T(8,128)}), f32[16,2,8,1024]{3,2,1,0:T(8,128)}) %reduce-scatter.5.cloned.1.call-update) | async-done | bytes 1048592 | tf_op jit(solution)/shard_map/reduce_scatter | solution.py:24
  96.4 17.8 %fusion.50 = f32[2,8,1024]{2,1,0:T(8,128)S(1)} fusion(f32[2,8,1024]{2,1,0:T(8,128)S(1)} %copy-done), kind=kOutput, calls=%fused_computation.67 | convolution fusion | flops 216006656 | bytes 131072 | tf_op jit(solution)/shard_map/dot_general | solution.py:113
  114.3 18.0 %broadcast_multiply_fusion = (f32[2,8,1024]{2,1,0:T(8,128)S(1)}, f32[2,8,1024]{2,1,0:T(8,128)S(1)}, f32[2,8,1024]{2,1,0:T(8,128)S(1)}, f32[2,8,1024]{2,1,0:T(8,128)S(1)}) fusion(f32[1024]{0:T(1024)S(1)} %get-tuple-element.358, f32[2,1024]{1,0:T(2,128)S(1)} %get-tuple-element.348, f32[2,8,1024]{2,1,0:T(8,128)S(1)} %fusion.50, ...), kind=kOutput, calls=%fused_computation.102 | convolution fusion | flops 216154112 | bytes 417792 | tf_op jit(solution)/shard_map/dot_general | solution.py:114
  132.3 18.4 %fusion.24 = f32[32,1024]{1,0:T(8,128)S(1)} fusion(f32[2,8,1024]{2,1,0:T(8,128)S(1)} %get-tuple-element.345, f32[2,8,1024]{2,1,0:T(8,128)S(1)} %get-tuple-element.324), kind=kOutput, calls=%fused_computation.53 | convolution fusion | flops 417366016 | bytes 262144 | tf_op jit(solution)/shard_map/dot_general | solution.py:121
  150.7 18.0 %fusion.47 = f32[32,1024]{1,0:T(8,128)S(1)} fusion(f32[32,1024]{1,0:T(8,128)S(1)} %fusion.24, f32[2,8,1024]{2,1,0:T(8,128)S(1)} %get-tuple-element.323, f32[2,8,1024]{2,1,0:T(8,128)S(1)} %get-tuple-element.346), kind=kOutput, calls=%fused_computation.66 | convolution fusion | flops 417431552 | bytes 393216 | tf_op jit(solution)/shard_map/dot_general | solution.py:122
  170.0 34.9 %all_gather.20 = bf16[16,2,8,1024]{3,2,1,0:T(8,128)(2,1)} all-gather(bf16[1,2,8,1024]{3,2,1,0:T(8,128)(2,1)S(1)} %fusion.69), channel_id=1, replica_groups=mesh['grp'=2,'slab_0'=16,'slab_1'=2,'ang'=4] {'slab_0'}, dimensions={0}, use_global_device_ids=true | all-gather | bytes 557056 | tf_op jit(solution)/shard_map/all_gather | solution.py:48
  205.3 15.5 %all-gather.5.cloned.1.call-done = bf16[32,2,8,1024]{3,2,1,0:T(8,128)(2,1)} async-done(((bf16[16,2,8,1024]{3,2,1,0:T(8,128)(2,1)}), bf16[32,2,8,1024]{3,2,1,0:T(8,128)(2,1)}) %all-gather.5.cloned.1.call-update) | async-done | bytes 1048592 | tf_op jit(solution)/shard_map/all_gather | solution.py:48
  223.0 4.2 fusion.10
  227.8 3.5 add_convert_fusion.1
  231.3 42.2 %all-reduce.6 = f32[2,256,1024]{2,1,0:T(8,128)S(1)} all-reduce(bf16[2,256,1024]{2,1,0:T(8,128)(2,1)S(1)} %bitcast.233), channel_id=1, replica_groups=mesh['grp'=2,'slab_0'=16,'slab_1'=2,'ang'=4] {'ang'}, use_global_device_ids=true, to_apply=%region_6.7 | all-reduce | flops 524288 | bytes 3145728 | tf_op jit(solution)/shard_map/psum | solution.py:96
  281.5 17.7 %while.14 = (s32[]{:T(128)}, f32[2,264,1024]{2,1,0:T(8,128)S(1)}, s32[2,3]{1,0:T(2,128)S(1)}, f32[2,256,1024]{2,1,0:T(8,128)}, s32[]{:T(128)}, /*index=5*/s32[3]{0:T(128)S(1)}, s32[]{:T(128)}) while((s32[]{:T(128)}, f32[2,264,1024]{2,1,0:T(8,128)S(1)}, s32[2,3]{1,0:T(2,128)S(1)}, f32[2,256,1024]{2,1,0:T(8,128)}, s32[]{:T(128)}, ...), condition=%wide.while_cond.6, body=%wide.while_body.6.sunk | while | flops 262163 | bytes 5243051 | solution.py:71
  293.7 3.3 dynamic-slice_select_fusion.10
  300.7 18.1 %while.15 = (s32[]{:T(128)}, f32[2,264,1024]{2,1,0:T(8,128)S(1)}, s32[2,3]{1,0:T(2,128)S(1)}, f32[2,256,1024]{2,1,0:T(8,128)}, s32[]{:T(128)}, /*index=5*/s32[3]{0:T(128)S(1)}, s32[]{:T(128)}) while((s32[]{:T(128)}, f32[2,264,1024]{2,1,0:T(8,128)S(1)}, s32[2,3]{1,0:T(2,128)S(1)}, f32[2,256,1024]{2,1,0:T(8,128)}, s32[]{:T(128)}, ...), condition=%wide.while_cond.7, body=%wide.while_body.7.sunk | while | flops 262163 | bytes 5243051 | solution.py:71
  304.2 3.4 dynamic-slice_select_fusion.11
  313.2 3.4 dynamic-slice_select_fusion.11
  322.2 20.0 %reduce-scatter.9.cloned.1.call-done = f32[16,2,8,1024]{3,2,1,0:T(8,128)} async-done(((f32[32,2,8,1024]{3,2,1,0:T(8,128)}), f32[16,2,8,1024]{3,2,1,0:T(8,128)}) %reduce-scatter.9.cloned.1.call-update) | async-done | bytes 1048592 | tf_op jit(solution)/shard_map/reduce_scatter | solution.py:24
  342.3 73.3 %reduce-scatter.11.cloned.1.call-done = f32[1,2,8,1024]{3,2,1,0:T(8,128)} async-done(((f32[16,2,8,1024]{3,2,1,0:T(8,128)}), f32[1,2,8,1024]{3,2,1,0:T(8,128)}) %reduce-scatter.11.cloned.1.call-update) | async-done | bytes 65552 | tf_op jit(solution)/shard_map/reduce_scatter | solution.py:24
  416.4 32.8 %all_gather.23 = bf16[16,2,8,1024]{3,2,1,0:T(8,128)(2,1)} all-gather(bf16[1,2,8,1024]{3,2,1,0:T(8,128)(2,1)S(1)} %fusion.70), channel_id=1, replica_groups=mesh['grp'=2,'slab_0'=16,'slab_1'=2,'ang'=4] {'slab_0'}, dimensions={0}, use_global_device_ids=true | all-gather | bytes 557056 | tf_op jit(solution)/shard_map/all_gather | solution.py:48
  451.4 10.5 %all-to-all-start = ((f32[32,1,2]{2,1,0:T(1,128)}), f32[32,1,2]{2,1,0:T(1,128)S(1)}, u32[]{:S(2)}, u32[]{:S(2)}) async-start(f32[32,1,2]{2,1,0:T(1,128)} %broadcast_in_dim.7), calls=%async_computation.4 | async-start | bytes 32768 | tf_op jit(solution)/shard_map/all_to_all | solution.py:61
  461.9 12.1 %all-to-all-done = f32[32,1,2]{2,1,0:T(1,128)S(1)} async-done(((f32[32,1,2]{2,1,0:T(1,128)}), f32[32,1,2]{2,1,0:T(1,128)S(1)}, u32[]{:S(2)}, u32[]{:S(2)}) %all-to-all-start) | async-done | bytes 288 | tf_op jit(solution)/shard_map/all_to_all | solution.py:61
  476.7 4.2 fusion.12
  481.5 4.5 add_convert_fusion
  486.0 42.0 %all-reduce.7 = f32[2,256,1024]{2,1,0:T(8,128)S(1)} all-reduce(bf16[2,256,1024]{2,1,0:T(8,128)(2,1)} %bitcast.234), channel_id=1, replica_groups=mesh['grp'=2,'slab_0'=16,'slab_1'=2,'ang'=4] {'ang'}, use_global_device_ids=true, to_apply=%region_13.14 | all-reduce | flops 524288 | bytes 3145728 | tf_op jit(solution)/shard_map/psum | solution.py:96
  (138 shorter events, 79.4 us)
Async XLA Ops:
  7.2 89.2 %copy-start = (f32[2,8,1024]{2,1,0:T(8,128)S(1)}, f32[2,8,1024]{2,1,0:T(8,128)}, u32[]{:S(2)}) copy-start(f32[2,8,1024]{2,1,0:T(8,128)} %param.8) | copy-start | bytes 196612
  7.2 88.6 %reduce-scatter.5.cloned.1.call-start = ((), (), s32[]{:S(2)}) async-start(), calls=%async_computation.5 | async-start | bytes 3145728 | tf_op jit(solution)/shard_map/reduce_scatter | solution.py:24
  7.3 4.7 copy-start.5
  7.3 4.7 copy-start.10
  12.0 2.6 copy-start.7
  12.0 2.7 copy-start.8
  14.6 0.7 copy-start.6
  63.1 33.1 %copy-start.9 = (f32[2]{0:T(128)S(1)}, f32[2]{0:T(128)}, u32[]{:S(2)}) copy-start(f32[2]{0:T(128)} %param.9) | copy-start | bytes 28
  63.2 106.0 %reduce-scatter.7.cloned.1.call-start = ((), (), s32[]{:S(2)}) async-start(), calls=%async_computation.6 | async-start | bytes 1114112 | tf_op jit(solution)/shard_map/reduce_scatter | solution.py:24
  95.8 124.9 %all-gather.5.cloned.1.call-start = ((), (), s32[]{:S(2)}) async-start(), calls=%async_computation.9 | async-start | bytes 1572864 | tf_op jit(solution)/shard_map/all_gather | solution.py:48
  205.0 137.2 %reduce-scatter.9.cloned.1.call-start = ((), (), s32[]{:S(2)}) async-start(), calls=%async_computation.7 | async-start | bytes 3145728 | tf_op jit(solution)/shard_map/reduce_scatter | solution.py:24
  273.5 2.5 copy-start.11
  276.0 2.6 copy-start.3
  319.0 1.2 copy-start.2
  322.1 93.5 %reduce-scatter.11.cloned.1.call-start = ((), (), s32[]{:S(2)}) async-start(), calls=%async_computation.8 | async-start | bytes 1114112 | tf_op jit(solution)/shard_map/reduce_scatter | solution.py:24
  342.3 132.4 %all-gather.7.cloned.1.call-start = ((), (), s32[]{:S(2)}) async-start(), calls=%async_computation.10 | async-start | bytes 1572864 | tf_op jit(solution)/shard_map/all_gather | solution.py:48
  451.4 22.6 %all-to-all-start = ((f32[32,1,2]{2,1,0:T(1,128)}), f32[32,1,2]{2,1,0:T(1,128)S(1)}, u32[]{:S(2)}, u32[]{:S(2)}) async-start(f32[32,1,2]{2,1,0:T(1,128)} %broadcast_in_dim.7), calls=%async_computation.4 | async-start | bytes 32768 | tf_op jit(solution)/shard_map/all_to_all | solution.py:61
  486.0 42.0 %copy-start.4 = (bf16[2,256,1024]{2,1,0:T(8,128)(2,1)S(1)}, bf16[2,256,1024]{2,1,0:T(8,128)(2,1)}, u32[]{:S(2)}) copy-start(bf16[2,256,1024]{2,1,0:T(8,128)(2,1)} %copy-done.3) | copy-start | bytes 3145732
  486.0 43.4 %copy-start.1 = (f32[2,8,1024]{2,1,0:T(8,128)S(1)}, f32[2,8,1024]{2,1,0:T(8,128)}, u32[]{:S(2)}) copy-start(f32[2,8,1024]{2,1,0:T(8,128)} %param.8) | copy-start | bytes 196612
Sparse Core Ops, SparseCore 0:
  63.3 32.4 reduce-scatter.4
  98.3 70.8 reduce-scatter.6
  205.1 15.5 all-gather.4
  322.2 19.9 reduce-scatter.8
  344.6 70.9 reduce-scatter.10
  449.5 16.1 all-gather.6
where the time goes:
time: 542 us; the launch traced here: 536 us
  waiting for transfers between devices  154 us (28%)
  blocking collectives  152 us (28%)
  matrix products  101 us (19%)
  other arithmetic  59.6 us (11%)
  local copies, waits for them, and re-layouts  43 us (8%)
  between operations  14.8 us (3%)
  starting transfers between devices  11.1 us (2%)
    reduce_scatter x4, waiting for transfers between devices, own_block(): tiles = lax.psum_scatter(tiles, axes[k], scatter_dimension=0, tiled=True)  126 us
    psum x2, blocking collectives, apply_update(): gradient = lax.psum(partial_wide, 'ang')  84.2 us
    all_gather x2, blocking collectives, stacked_from(): tiles = lax.all_gather(tiles, axes[k])  67.7 us
    scatter x16, other arithmetic  49.3 us
    scatter x24, local copies, waits for them, and re-layouts  28.3 us
    dot_general x1, matrix products, per_device(): jnp.dot(first_half, cosine, precision=highest)  18.4 us
    dot_general x1, matrix products, per_device(): jnp.dot(flat_rows, sine, precision=highest)  18 us
    dot_general x1, matrix products, per_device(): jnp.dot(second_half, sine, precision=highest)  18 us
  transfers between devices with their start and end apart: 7, of which 6 were waited for; matrix products, arithmetic and copies ran while one was open for 14% of the time, Pallas kernels for 0%

commit v1 on v0

--- a/solution.py
+++ b/solution.py
@@ -93,7 +93,7 @@
 def apply_update(current, running):
     partial_value = lax.optimization_barrier(running.reshape(current.shape).astype(jnp.bfloat16))
     partial_wide = partial_value.astype(jnp.float32)
-    gradient = lax.psum(partial_wide, "ang")
+    gradient = jnp.sum(lax.all_gather(partial_wide, "ang"), axis=0)
     renewed = (current.astype(jnp.float32) - step_size * gradient).astype(jnp.bfloat16)
     return renewed
 

time: 542 us -> 639 us (1.18)
  waiting for transfers between devices: 154 us -> 313 us
  blocking collectives: 152 us -> 92.6 us
  starting transfers between devices: 11.1 us -> 0.8 us
  other arithmetic: 59.6 us -> 67.7 us
    all_gather x0 -> x2, waiting for transfers between devices: none -> 155 us  [apply_update(): gradient = jnp.sum(lax.all_gather(partial_wide, 'ang'), axis=0)]
    psum x2 -> x0, blocking collectives: 84.2 us -> none  [apply_update(): gradient = lax.psum(partial_wide, 'ang')]
    all_to_all x0 -> x1, blocking collectives: none -> 24.7 us  [from_everyone(): return lax.all_to_all(copies, axis, split_axis=0, concat_axis=0, tiled=True)]
    all_gather x2, waiting for transfers between devices: 15.5 us -> 31.9 us  [stacked_from(): tiles = lax.all_gather(tiles, axes[k])]
    all_to_all x1 -> x0, waiting for transfers between devices: 12.1 us -> none  [from_everyone(): return lax.all_to_all(copies, axis, split_axis=0, concat_axis=0, tiled=True)]
    all_to_all x1 -> x0, starting transfers between devices: 10.5 us -> none  [from_everyone(): return lax.all_to_all(copies, axis, split_axis=0, concat_axis=0, tiled=True)]
    reduce_sum x0 -> x2, other arithmetic: none -> 9.27 us  [apply_update(): gradient = jnp.sum(lax.all_gather(partial_wide, 'ang'), axis=0)]
  transfers between devices with their start and end apart: 7 -> 8, of which waited for: 6 -> 8; matrix products, arithmetic and copies ran while one was open for 14% -> 12% of each run, Pallas kernels for 0% -> 0%
where the time goes in v1:
time: 639 us; the launch traced here: 633 us
  waiting for transfers between devices  313 us (49%)
  matrix products  100 us (16%)
  blocking collectives  92.6 us (14%)
  other arithmetic  67.7 us (11%)
  local copies, waits for them, and re-layouts  42.6 us (7%)
  between operations  14.8 us (2%)
    all_gather x2, waiting for transfers between devices, apply_update(): gradient = jnp.sum(lax.all_gather(partial_wide, 'ang'), axis=0)  155 us
    reduce_scatter x4, waiting for transfers between devices, own_block(): tiles = lax.psum_scatter(tiles, axes[k], scatter_dimension=0, tiled=True)  126 us
    all_gather x2, blocking collectives, stacked_from(): tiles = lax.all_gather(tiles, axes[k])  67.9 us
    scatter x16, other arithmetic  47.1 us
    all_gather x2, waiting for transfers between devices, stacked_from(): tiles = lax.all_gather(tiles, axes[k])  31.9 us
    scatter x24, local copies, waits for them, and re-layouts  27.4 us
    all_to_all x1, blocking collectives, from_everyone(): return lax.all_to_all(copies, axis, split_axis=0, concat_axis=0, tiled=True)  24.7 us
    dot_general x1, matrix products, per_device(): jnp.dot(first_half, cosine, precision=highest)  18.4 us
  transfers between devices with their start and end apart: 8, of which 8 were waited for; matrix products, arithmetic and copies ran while one was open for 12% of the time, Pallas kernels for 0%

profile of v1, /device:TPU:34, one launch (start us, length us, event | category | flops | bytes accessed | tf_op | source)
XLA Modules:
  0.0 632.9 jit_solution(16713878553001837276)
XLA Ops:
  7.3 4.6 fusion.16
  15.2 16.5 %while.12 = (s32[]{:T(128)}, f32[2,264,1024]{2,1,0:T(8,128)S(1)}, s32[2,3]{1,0:T(2,128)S(1)}, f32[2,256,1024]{2,1,0:T(8,128)}, s32[]{:T(128)}, /*index=5*/s32[3]{0:T(128)S(1)}, s32[]{:T(128)}) while((s32[]{:T(128)}, f32[2,264,1024]{2,1,0:T(8,128)S(1)}, s32[2,3]{1,0:T(2,128)S(1)}, f32[2,256,1024]{2,1,0:T(8,128)}, s32[]{:T(128)}, ...), condition=%wide.while_cond.4, body=%wide.while_body.4.sunk | while | flops 262163 | bytes 5243051 | solution.py:71
  18.3 3.1 dynamic-slice_select_fusion.8
  33.4 24.2 %while.13 = (s32[]{:T(128)}, f32[2,264,1024]{2,1,0:T(8,128)}, s32[2,3]{1,0:T(2,128)S(1)}, f32[2,256,1024]{2,1,0:T(8,128)}, s32[]{:T(128)}, /*index=5*/s32[3]{0:T(128)S(1)}, s32[]{:T(128)}) while((s32[]{:T(128)}, f32[2,264,1024]{2,1,0:T(8,128)}, s32[2,3]{1,0:T(2,128)S(1)}, f32[2,256,1024]{2,1,0:T(8,128)}, s32[]{:T(128)}, /*index=5*/s32[3]{0:T(128)S(1)}, ...), condition=%wide.while_cond.5, body=%wide.while_body.5.sunk | while | flops 262163 | bytes 5243051 | solution.py:71
  36.7 3.7 dynamic-slice_select_fusion.9
  40.4 5.1 dynamic-update-slice.33
  48.8 3.7 dynamic-slice_select_fusion.9
  52.5 5.1 dynamic-update-slice.33
  61.8 32.5 %reduce-scatter.5.cloned.1.call-done = f32[16,2,8,1024]{3,2,1,0:T(8,128)} async-done(((f32[32,2,8,1024]{3,2,1,0:T(8,128)}), f32[16,2,8,1024]{3,2,1,0:T(8,128)}) %reduce-scatter.5.cloned.1.call-update) | async-done | bytes 1048592 | tf_op jit(solution)/shard_map/reduce_scatter | solution.py:24
  95.0 17.8 %fusion.50 = f32[2,8,1024]{2,1,0:T(8,128)S(1)} fusion(f32[2,8,1024]{2,1,0:T(8,128)S(1)} %copy-done), kind=kOutput, calls=%fused_computation.67 | convolution fusion | flops 216006656 | bytes 131072 | tf_op jit(solution)/shard_map/dot_general | solution.py:113
  112.8 18.0 %broadcast_multiply_fusion = (f32[2,8,1024]{2,1,0:T(8,128)S(1)}, f32[2,8,1024]{2,1,0:T(8,128)S(1)}, f32[2,8,1024]{2,1,0:T(8,128)S(1)}, f32[2,8,1024]{2,1,0:T(8,128)S(1)}) fusion(f32[1024]{0:T(1024)S(1)} %get-tuple-element.358, f32[2,1024]{1,0:T(2,128)S(1)} %get-tuple-element.348, f32[2,8,1024]{2,1,0:T(8,128)S(1)} %fusion.50, ...), kind=kOutput, calls=%fused_computation.102 | convolution fusion | flops 216154112 | bytes 417792 | tf_op jit(solution)/shard_map/dot_general | solution.py:114
  130.8 18.4 %fusion.24 = f32[32,1024]{1,0:T(8,128)S(1)} fusion(f32[2,8,1024]{2,1,0:T(8,128)S(1)} %get-tuple-element.345, f32[2,8,1024]{2,1,0:T(8,128)S(1)} %get-tuple-element.324), kind=kOutput, calls=%fused_computation.53 | convolution fusion | flops 417366016 | bytes 262144 | tf_op jit(solution)/shard_map/dot_general | solution.py:121
  149.3 18.0 %fusion.47 = f32[32,1024]{1,0:T(8,128)S(1)} fusion(f32[32,1024]{1,0:T(8,128)S(1)} %fusion.24, f32[2,8,1024]{2,1,0:T(8,128)S(1)} %get-tuple-element.323, f32[2,8,1024]{2,1,0:T(8,128)S(1)} %get-tuple-element.346), kind=kOutput, calls=%fused_computation.66 | convolution fusion | flops 417431552 | bytes 393216 | tf_op jit(solution)/shard_map/dot_general | solution.py:122
  168.6 34.9 %all_gather.38 = bf16[16,2,8,1024]{3,2,1,0:T(8,128)(2,1)} all-gather(bf16[1,2,8,1024]{3,2,1,0:T(8,128)(2,1)S(1)} %fusion.69), channel_id=1, replica_groups=mesh['grp'=2,'slab_0'=16,'slab_1'=2,'ang'=4] {'slab_0'}, dimensions={0}, use_global_device_ids=true | all-gather | bytes 557056 | tf_op jit(solution)/shard_map/all_gather | solution.py:48
  203.8 15.5 %all-gather.9.cloned.1.call-done = bf16[32,2,8,1024]{3,2,1,0:T(8,128)(2,1)} async-done(((bf16[16,2,8,1024]{3,2,1,0:T(8,128)(2,1)}), bf16[32,2,8,1024]{3,2,1,0:T(8,128)(2,1)}) %all-gather.9.cloned.1.call-update) | async-done | bytes 1048592 | tf_op jit(solution)/shard_map/all_gather | solution.py:48
  221.5 4.2 fusion.10
  226.3 3.5 add_convert_fusion.1
  231.6 90.5 %all-gather.11.cloned.1.call-done = f32[8,256,1024]{2,1,0:T(8,128)} async-done(((f32[2,256,1024]{2,1,0:T(8,128)}), f32[8,256,1024]{2,1,0:T(8,128)}) %all-gather.11.cloned.1.call-update) | async-done | bytes 8388624 | tf_op jit(solution)/shard_map/all_gather | solution.py:96
  322.1 4.6 reduce_sum.74
  334.4 17.6 %while.14 = (s32[]{:T(128)}, f32[2,264,1024]{2,1,0:T(8,128)S(1)}, s32[2,3]{1,0:T(2,128)S(1)}, f32[2,256,1024]{2,1,0:T(8,128)}, s32[]{:T(128)}, /*index=5*/s32[3]{0:T(128)S(1)}, s32[]{:T(128)}) while((s32[]{:T(128)}, f32[2,264,1024]{2,1,0:T(8,128)S(1)}, s32[2,3]{1,0:T(2,128)S(1)}, f32[2,256,1024]{2,1,0:T(8,128)}, s32[]{:T(128)}, ...), condition=%wide.while_cond.6, body=%wide.while_body.6.sunk | while | flops 262163 | bytes 5243051 | solution.py:71
  337.7 3.3 dynamic-slice_select_fusion.10
  346.5 3.3 dynamic-slice_select_fusion.10
  353.6 16.5 %while.15 = (s32[]{:T(128)}, f32[2,264,1024]{2,1,0:T(8,128)S(1)}, s32[2,3]{1,0:T(2,128)S(1)}, f32[2,256,1024]{2,1,0:T(8,128)}, s32[]{:T(128)}, /*index=5*/s32[3]{0:T(128)S(1)}, s32[]{:T(128)}) while((s32[]{:T(128)}, f32[2,264,1024]{2,1,0:T(8,128)S(1)}, s32[2,3]{1,0:T(2,128)S(1)}, f32[2,256,1024]{2,1,0:T(8,128)}, s32[]{:T(128)}, ...), condition=%wide.while_cond.7, body=%wide.while_body.7.sunk | while | flops 262163 | bytes 5243051 | solution.py:71
  373.4 19.8 %reduce-scatter.9.cloned.1.call-done = f32[16,2,8,1024]{3,2,1,0:T(8,128)} async-done(((f32[32,2,8,1024]{3,2,1,0:T(8,128)}), f32[16,2,8,1024]{3,2,1,0:T(8,128)}) %reduce-scatter.9.cloned.1.call-update) | async-done | bytes 1048592 | tf_op jit(solution)/shard_map/reduce_scatter | solution.py:24
  393.4 73.2 %reduce-scatter.11.cloned.1.call-done = f32[1,2,8,1024]{3,2,1,0:T(8,128)} async-done(((f32[16,2,8,1024]{3,2,1,0:T(8,128)}), f32[1,2,8,1024]{3,2,1,0:T(8,128)}) %reduce-scatter.11.cloned.1.call-update) | async-done | bytes 65552 | tf_op jit(solution)/shard_map/reduce_scatter | solution.py:24
  467.5 33.0 %all_gather.44 = bf16[16,2,8,1024]{3,2,1,0:T(8,128)(2,1)} all-gather(bf16[1,2,8,1024]{3,2,1,0:T(8,128)(2,1)S(1)} %fusion.70), channel_id=1, replica_groups=mesh['grp'=2,'slab_0'=16,'slab_1'=2,'ang'=4] {'slab_0'}, dimensions={0}, use_global_device_ids=true | all-gather | bytes 557056 | tf_op jit(solution)/shard_map/all_gather | solution.py:48
  500.6 16.4 %all-gather.13.cloned.1.call-done = bf16[32,2,8,1024]{3,2,1,0:T(8,128)(2,1)} async-done(((bf16[16,2,8,1024]{3,2,1,0:T(8,128)(2,1)}), bf16[32,2,8,1024]{3,2,1,0:T(8,128)(2,1)}) %all-gather.13.cloned.1.call-update) | async-done | bytes 1048592 | tf_op jit(solution)/shard_map/all_gather | solution.py:48
  519.2 4.2 fusion.12
  524.0 3.5 add_convert_fusion
  529.9 24.7 %all_to_all.6 = f32[32,1,2]{2,1,0:T(1,128)S(1)} all-to-all(f32[32,1,2]{2,1,0:T(1,128)S(1)} %broadcast_in_dim.7), channel_id=1, replica_groups=mesh['grp'=2,'slab_0'=16,'slab_1'=2,'ang'=4] {'slab_0','slab_1'}, dimensions={0} | all-to-all | bytes 512 | tf_op jit(solution)/shard_map/all_to_all | solution.py:61
  555.2 64.6 %all-gather.15.cloned.1.call-done = f32[8,256,1024]{2,1,0:T(8,128)} async-done(((f32[2,256,1024]{2,1,0:T(8,128)}), f32[8,256,1024]{2,1,0:T(8,128)}) %all-gather.15.cloned.1.call-update) | async-done | bytes 8388624 | tf_op jit(solution)/shard_map/all_gather | solution.py:96
  619.8 4.6 reduce_sum.77
  (149 shorter events, 85.2 us)
Async XLA Ops:
  7.2 87.8 %copy-start = (f32[2,8,1024]{2,1,0:T(8,128)S(1)}, f32[2,8,1024]{2,1,0:T(8,128)}, u32[]{:S(2)}) copy-start(f32[2,8,1024]{2,1,0:T(8,128)} %param.8) | copy-start | bytes 196612
  7.2 87.1 %reduce-scatter.5.cloned.1.call-start = ((), (), s32[]{:S(2)}) async-start(), calls=%async_computation.5 | async-start | bytes 3145728 | tf_op jit(solution)/shard_map/reduce_scatter | solution.py:24
  7.3 4.7 copy-start.5
  7.3 4.7 copy-start.12
  11.9 2.6 copy-start.9
  11.9 2.7 copy-start.10
  14.6 0.7 copy-start.8
  61.7 33.1 %copy-start.11 = (f32[2]{0:T(128)S(1)}, f32[2]{0:T(128)}, u32[]{:S(2)}) copy-start(f32[2]{0:T(128)} %param.9) | copy-start | bytes 28
  61.7 106.0 %reduce-scatter.7.cloned.1.call-start = ((), (), s32[]{:S(2)}) async-start(), calls=%async_computation.6 | async-start | bytes 1114112 | tf_op jit(solution)/shard_map/reduce_scatter | solution.py:24
  94.4 124.9 %all-gather.9.cloned.1.call-start = ((), (), s32[]{:S(2)}) async-start(), calls=%async_computation.9 | async-start | bytes 1572864 | tf_op jit(solution)/shard_map/all_gather | solution.py:48
  203.5 118.6 %all-gather.11.cloned.1.call-start = ((), (), s32[]{:S(2)}) async-start(), calls=%async_computation.10 | async-start | bytes 10485760 | tf_op jit(solution)/shard_map/all_gather | solution.py:96
  231.5 161.7 %reduce-scatter.9.cloned.1.call-start = ((), (), s32[]{:S(2)}) async-start(), calls=%async_computation.7 | async-start | bytes 3145728 | tf_op jit(solution)/shard_map/reduce_scatter | solution.py:24
  322.1 4.6 copy-start.6
  326.7 2.2 copy-start.13
  328.9 2.6 copy-start.3
  370.3 1.2 copy-start.2
  373.3 93.3 %reduce-scatter.11.cloned.1.call-start = ((), (), s32[]{:S(2)}) async-start(), calls=%async_computation.8 | async-start | bytes 1114112 | tf_op jit(solution)/shard_map/reduce_scatter | solution.py:24
  393.3 123.7 %all-gather.13.cloned.1.call-start = ((), (), s32[]{:S(2)}) async-start(), calls=%async_computation.11 | async-start | bytes 1572864 | tf_op jit(solution)/shard_map/all_gather | solution.py:48
  500.5 119.3 %all-gather.15.cloned.1.call-start = ((), (), s32[]{:S(2)}) async-start(), calls=%async_computation.12 | async-start | bytes 10485760 | tf_op jit(solution)/shard_map/all_gather | solution.py:96
  527.5 1.7 copy-start.7
  619.8 4.6 copy-start.4
  619.8 6.0 copy-start.1
Sparse Core Ops, SparseCore 0:
  61.9 32.4 reduce-scatter.4
  96.8 70.8 reduce-scatter.6
  203.6 15.6 all-gather.8
  231.6 90.4 all-gather.10
  373.5 19.7 reduce-scatter.8
  395.6 70.9 reduce-scatter.10
  500.6 16.2 all-gather.12
  529.3 90.4 all-gather.14
